TPU v7x, 32 devices: a whole 2x2x4 slice. The times are simulated.
32 devices in a mesh: pairs: 2 (over y), aa: 4 (over z), ba: 4 (over x, core).
Axes of the slice: x: 2, y: 2, z: 4, core: 2. Of those that a mesh axis runs over, the one named last changes fastest.
Arguments:
- feats_a: float32 [1024, 256], P(('pairs', 'aa', 'ba')), parts along dimension 0, may hold values from -24 to 24
- feats_b: float32 [512, 256], P(('pairs', 'ba', 'aa')), parts along dimension 0, may hold values from -24 to 24
- qk_weight: float32 [2, 256, 256], replicated, may hold values from -0.375 to 0.375
- qk_bias: float32 [2, 256], replicated, may hold values from -3 to 3
- value_weight: float32 [2, 256, 256], replicated, may hold values from -0.375 to 0.375
- value_bias: float32 [2, 256], replicated, may hold values from -3 to 3
- out_weight: float32 [2, 256, 256], replicated, may hold values from -0.375 to 0.375
- out_bias: float32 [2, 256], replicated, may hold values from -3 to 3
- hidden_weight: float32 [2, 512, 512], replicated, may hold values from -0.25 to 0.25
- hidden_bias: float32 [2, 512], replicated, may hold values from -3 to 3
- norm_gain: float32 [2, 512], replicated, may hold values from 0.25 to 1.75
- norm_bias: float32 [2, 512], replicated, may hold values from -3 to 3
- final_weight: float32 [2, 512, 256], replicated, may hold values from -0.25 to 0.25
- final_bias: float32 [2, 256], replicated, may hold values from -3 to 3
Outputs:
- out_a: float32 [1024, 256], P(('pairs', 'aa', 'ba')), parts along dimension 0
- out_b: float32 [512, 256], P(('pairs', 'ba', 'aa')), parts along dimension 0
There are 2 independent parts, one for each index of `pairs`. A program takes and returns all parts, laid end to end along the dimension named above; an argument that names none is the same for every part. Nothing has to cross between parts.
All inputs are finite; a program needn't handle non-finite values.
Results may differ from a plain program's by a relative error of at most 0.0003.
Values sent between devices are 32-bit elements; how exact they have to be, the bound alone decides.
A program may use at most 64 MiB of HBM per device.

v0:
```python
import jax
import jax.numpy as jnp
from jax import lax
from jax.sharding import PartitionSpec as P

HEADS = 4


EXACT_RESULT = lax.Precision.HIGHEST


def matmul(left, right):
    return jnp.dot(left, right, precision=EXACT_RESULT)


def layer_norm(values, gain, offset):
    average = jnp.mean(values, -1, keepdims=True)
    centred = values - average
    spread = jnp.mean(centred * centred, -1, keepdims=True)
    return centred / jnp.sqrt(spread + 1e-05) * gain + offset


def feed_forward(
    state, message, hidden_weight, hidden_bias, norm_gain, norm_bias, final_weight, final_bias
):
    joined = jnp.concatenate([state, message], -1)
    hidden = matmul(joined, hidden_weight) + hidden_bias
    active = jax.nn.gelu(layer_norm(hidden, norm_gain, norm_bias), approximate=False)
    return state + matmul(active, final_weight) + final_bias


def settle_owner(numer, tops, totals):
    best = jnp.max(tops, 0)
    weight = jnp.exp(tops - best[None])
    denom = jnp.sum(weight * totals, 0)
    sources = numer.shape[0]
    rows = numer.shape[1]
    heads = tops.shape[2]
    shaped = numer.reshape(sources, rows, heads, -1)
    joined = jnp.sum(shaped * weight[:, :, :, None], 0) / denom[:, :, None]
    return joined.reshape(rows, -1)


def shards(
    feats_a,
    feats_b,
    qk_weight,
    qk_bias,
    value_weight,
    value_bias,
    out_weight,
    out_bias,
    hidden_weight,
    hidden_bias,
    norm_gain,
    norm_bias,
    final_weight,
    final_bias,
):
    width = feats_a.shape[1]
    head_count = HEADS
    head_width = width // head_count
    softmax_temper = head_width ** (-0.5)
    first = feats_a
    second = feats_b
    for layer_index in range(qk_weight.shape[0]):
        joint_weight = jnp.concatenate([qk_weight[layer_index], value_weight[layer_index]], 1)
        joint_bias = jnp.concatenate([qk_bias[layer_index], value_bias[layer_index]], 0)
        proj_a = matmul(first, joint_weight) + joint_bias
        proj_b = matmul(second, joint_weight) + joint_bias
        block_a = lax.all_gather(proj_a, "ba", axis=0, tiled=True)
        block_b = lax.all_gather(proj_b, "aa", axis=0, tiled=True)
        query_first_image = block_a[:, :width].reshape(-1, head_count, head_width)
        value_a = block_a[:, width:].reshape(-1, head_count, head_width)
        query_second_image = block_b[:, :width].reshape(-1, head_count, head_width)
        value_b = block_b[:, width:].reshape(-1, head_count, head_width)
        score_matrix = (
            jnp.einsum(
                "cjg,xjg->jcx", query_first_image, query_second_image, precision=EXACT_RESULT
            )
            * softmax_temper
        )
        row_local = jnp.max(score_matrix, 2)
        col_local = jnp.max(score_matrix, 1)
        row_exp = jnp.exp(score_matrix - row_local[:, :, None])
        col_exp = jnp.exp(score_matrix - col_local[:, None, :])
        numer_a = jnp.einsum("hab,bhd->ahd", row_exp, value_b, precision=EXACT_RESULT).reshape(
            -1, width
        )
        numer_b = jnp.einsum("hab,ahd->bhd", col_exp, value_a, precision=EXACT_RESULT).reshape(
            -1, width
        )
        row_tops = jnp.transpose(row_local)
        row_totals = jnp.transpose(jnp.sum(row_exp, 2))
        col_tops = jnp.transpose(col_local)
        col_totals = jnp.transpose(jnp.sum(col_exp, 1))
        arrived_a = (
            lax.all_to_all(numer_a[None], "ba", split_axis=1, concat_axis=0, tiled=True),
            lax.all_to_all(row_tops[None], "ba", split_axis=1, concat_axis=0, tiled=True),
            lax.all_to_all(row_totals[None], "ba", split_axis=1, concat_axis=0, tiled=True),
        )
        arrived_b = (
            lax.all_to_all(numer_b[None], "aa", split_axis=1, concat_axis=0, tiled=True),
            lax.all_to_all(col_tops[None], "aa", split_axis=1, concat_axis=0, tiled=True),
            lax.all_to_all(col_totals[None], "aa", split_axis=1, concat_axis=0, tiled=True),
        )
        msg_a = settle_owner(arrived_a[0], arrived_a[1], arrived_a[2])
        msg_b = settle_owner(arrived_b[0], arrived_b[1], arrived_b[2])
        reply_a = matmul(msg_a, out_weight[layer_index]) + out_bias[layer_index]
        reply_b = matmul(msg_b, out_weight[layer_index]) + out_bias[layer_index]
        first = feed_forward(
            first,
            reply_a,
            hidden_weight[layer_index],
            hidden_bias[layer_index],
            norm_gain[layer_index],
            norm_bias[layer_index],
            final_weight[layer_index],
            final_bias[layer_index],
        )
        second = feed_forward(
            second,
            reply_b,
            hidden_weight[layer_index],
            hidden_bias[layer_index],
            norm_gain[layer_index],
            norm_bias[layer_index],
            final_weight[layer_index],
            final_bias[layer_index],
        )
    return (first, second)


def solution(mesh):
    in_specs = (
        P(("pairs", "aa", "ba"), None),
        P(("pairs", "ba", "aa"), None),
        P(),
        P(),
        P(),
        P(),
        P(),
        P(),
        P(),
        P(),
        P(),
        P(),
        P(),
        P(),
    )
    out_specs = (P(("pairs", "aa", "ba"), None), P(("pairs", "ba", "aa"), None))
    return jax.shard_map(shards, mesh=mesh, in_specs=in_specs, out_specs=out_specs, check_vma=False)
```

profile of v0, /device:TPU:0, one launch (start us, length us, event | category | flops | bytes accessed | tf_op | source)
XLA Modules:
  0.0 162.1 jit_solution(1731793218481683486)
XLA Ops:
  2.2 1.3 slice_bitcast_fusion
  3.9 15.1 %all_gather.12 = f32[64,512]{1,0:T(8,128)S(1)} all-gather(f32[16,512]{1,0:T(8,128)S(1)} %fusion.1), channel_id=1, replica_groups=mesh['pairs'=2,'aa'=4,'ba'=4] {'aa'}, dimensions={0}, use_global_device_ids=true | all-gather | bytes 163840 | tf_op jit(solution)/shard_map/all_gather | solution.py:72
  19.5 5.8 %all_gather.13 = f32[128,512]{1,0:T(8,128)S(1)} all-gather(f32[32,512]{1,0:T(8,128)S(1)} %fusion), channel_id=1, replica_groups=mesh['pairs'=2,'aa'=4,'ba'=4] {'ba'}, dimensions={0}, use_global_device_ids=true | all-gather | bytes 327680 | tf_op jit(solution)/shard_map/all_gather | solution.py:71
  28.1 3.2 %all-to-all-start.2 = ((f32[4,1,128]{2,1,0:T(1,128)}), f32[4,1,128]{2,1,0:T(1,128)S(1)}, u32[]{:S(2)}, u32[]{:S(2)}) async-start(f32[4,1,128]{2,1,0:T(1,128)} %reshape.316), calls=%async_computation.2 | async-start | bytes 4096 | tf_op jit(solution)/shard_map/all_to_all | solution.py:100
  35.6 3.2 %all-to-all-start.1 = ((f32[4,1,128]{2,1,0:T(1,128)}), f32[4,1,128]{2,1,0:T(1,128)S(1)}, u32[]{:S(2)}, u32[]{:S(2)}) async-start(f32[4,1,128]{2,1,0:T(1,128)} %reshape.314), calls=%async_computation.1 | async-start | bytes 4096 | tf_op jit(solution)/shard_map/all_to_all | solution.py:99
  40.1 2.4 %all-to-all-done.1 = f32[4,1,128]{2,1,0:T(1,128)S(1)} async-done(((f32[4,1,128]{2,1,0:T(1,128)}), f32[4,1,128]{2,1,0:T(1,128)S(1)}, u32[]{:S(2)}, u32[]{:S(2)}) %all-to-all-start.1) | async-done | bytes 2080 | tf_op jit(solution)/shard_map/all_to_all | solution.py:99
  42.5 5.0 %all-to-all-start.4 = ((f32[1,64,4]{2,0,1:T(1,128)}), f32[1,64,4]{2,0,1:T(1,128)S(1)}, u32[]{:S(2)}, u32[]{:S(2)}) async-start(f32[1,64,4]{2,0,1:T(1,128)} %copy.85), calls=%async_computation.4 | async-start | bytes 65536 | tf_op jit(solution)/shard_map/all_to_all | solution.py:104
  48.8 4.3 %all-to-all-done.4 = f32[1,64,4]{2,0,1:T(1,128)S(1)} async-done(((f32[1,64,4]{2,0,1:T(1,128)}), f32[1,64,4]{2,0,1:T(1,128)S(1)}, u32[]{:S(2)}, u32[]{:S(2)}) %all-to-all-start.4) | async-done | bytes 1056 | tf_op jit(solution)/shard_map/all_to_all | solution.py:104
  53.2 3.3 %all-to-all-start.5 = ((f32[1,64,4]{2,0,1:T(1,128)}), f32[1,64,4]{2,0,1:T(1,128)S(1)}, u32[]{:S(2)}, u32[]{:S(2)}) async-start(f32[1,64,4]{2,0,1:T(1,128)} %copy.89), calls=%async_computation.5 | async-start | bytes 65536 | tf_op jit(solution)/shard_map/all_to_all | solution.py:105
  60.4 1.7 %all-to-all-done.5 = f32[1,64,4]{2,0,1:T(1,128)S(1)} async-done(((f32[1,64,4]{2,0,1:T(1,128)}), f32[1,64,4]{2,0,1:T(1,128)S(1)}, u32[]{:S(2)}, u32[]{:S(2)}) %all-to-all-start.5) | async-done | bytes 1056 | tf_op jit(solution)/shard_map/all_to_all | solution.py:105
  62.1 3.9 %all-to-all-start = ((f32[1,128,256]{2,0,1:T(1,128)}), f32[1,128,256]{2,0,1:T(1,128)}, u32[]{:S(2)}, u32[]{:S(2)}) async-start(f32[1,128,256]{2,0,1:T(1,128)} %copy.75), calls=%async_computation | async-start | bytes 262144 | tf_op jit(solution)/shard_map/all_to_all | solution.py:98
  66.8 1.2 multiply_reduce_fusion.10
  68.5 1.4 copy.82
  70.9 1.3 copy.91
  72.3 3.4 %all-to-all-start.3 = ((f32[1,64,256]{2,0,1:T(1,128)}), f32[1,64,256]{2,0,1:T(1,128)S(1)}, u32[]{:S(2)}, u32[]{:S(2)}) async-start(f32[1,64,256]{2,0,1:T(1,128)} %copy.84), calls=%async_computation.3 | async-start | bytes 131072 | tf_op jit(solution)/shard_map/all_to_all | solution.py:103
  78.6 1.6 fusion.569
  82.9 1.6 fusion.2
  85.3 13.3 %all_gather.14 = f32[64,512]{1,0:T(8,128)S(1)} all-gather(f32[16,512]{1,0:T(8,128)S(1)} %convolution_add_fusion.9), channel_id=1, replica_groups=mesh['pairs'=2,'aa'=4,'ba'=4] {'aa'}, dimensions={0}, use_global_device_ids=true | all-gather | bytes 163840 | tf_op jit(solution)/shard_map/all_gather | solution.py:72
  99.1 6.3 %all_gather.15 = f32[128,512]{1,0:T(8,128)S(1)} all-gather(f32[32,512]{1,0:T(8,128)S(1)} %convolution_add_fusion.2), channel_id=1, replica_groups=mesh['pairs'=2,'aa'=4,'ba'=4] {'ba'}, dimensions={0}, use_global_device_ids=true | all-gather | bytes 327680 | tf_op jit(solution)/shard_map/all_gather | solution.py:71
  107.7 3.2 %all-to-all-start.8 = ((f32[4,1,128]{2,1,0:T(1,128)}), f32[4,1,128]{2,1,0:T(1,128)S(1)}, u32[]{:S(2)}, u32[]{:S(2)}) async-start(f32[4,1,128]{2,1,0:T(1,128)} %reshape.320), calls=%async_computation.8 | async-start | bytes 4096 | tf_op jit(solution)/shard_map/all_to_all | solution.py:100
  112.5 2.1 %all-to-all-done.8 = f32[4,1,128]{2,1,0:T(1,128)S(1)} async-done(((f32[4,1,128]{2,1,0:T(1,128)}), f32[4,1,128]{2,1,0:T(1,128)S(1)}, u32[]{:S(2)}, u32[]{:S(2)}) %all-to-all-start.8) | async-done | bytes 2080 | tf_op jit(solution)/shard_map/all_to_all | solution.py:100
  114.6 3.2 %all-to-all-start.7 = ((f32[4,1,128]{2,1,0:T(1,128)}), f32[4,1,128]{2,1,0:T(1,128)S(1)}, u32[]{:S(2)}, u32[]{:S(2)}) async-start(f32[4,1,128]{2,1,0:T(1,128)} %reshape.318), calls=%async_computation.7 | async-start | bytes 4096 | tf_op jit(solution)/shard_map/all_to_all | solution.py:99
  118.6 2.9 %all-to-all-done.7 = f32[4,1,128]{2,1,0:T(1,128)S(1)} async-done(((f32[4,1,128]{2,1,0:T(1,128)}), f32[4,1,128]{2,1,0:T(1,128)S(1)}, u32[]{:S(2)}, u32[]{:S(2)}) %all-to-all-start.7) | async-done | bytes 2080 | tf_op jit(solution)/shard_map/all_to_all | solution.py:99
  121.5 4.4 %all-to-all-start.10 = ((f32[1,64,4]{2,0,1:T(1,128)}), f32[1,64,4]{2,0,1:T(1,128)S(1)}, u32[]{:S(2)}, u32[]{:S(2)}) async-start(f32[1,64,4]{2,0,1:T(1,128)} %copy.105), calls=%async_computation.10 | async-start | bytes 65536 | tf_op jit(solution)/shard_map/all_to_all | solution.py:104
  127.0 4.6 %all-to-all-done.10 = f32[1,64,4]{2,0,1:T(1,128)S(1)} async-done(((f32[1,64,4]{2,0,1:T(1,128)}), f32[1,64,4]{2,0,1:T(1,128)S(1)}, u32[]{:S(2)}, u32[]{:S(2)}) %all-to-all-start.10) | async-done | bytes 1056 | tf_op jit(solution)/shard_map/all_to_all | solution.py:104
  131.6 3.3 %all-to-all-start.11 = ((f32[1,64,4]{2,0,1:T(1,128)}), f32[1,64,4]{2,0,1:T(1,128)S(1)}, u32[]{:S(2)}, u32[]{:S(2)}) async-start(f32[1,64,4]{2,0,1:T(1,128)} %copy.109), calls=%async_computation.11 | async-start | bytes 65536 | tf_op jit(solution)/shard_map/all_to_all | solution.py:105
  138.6 1.9 %all-to-all-done.11 = f32[1,64,4]{2,0,1:T(1,128)S(1)} async-done(((f32[1,64,4]{2,0,1:T(1,128)}), f32[1,64,4]{2,0,1:T(1,128)S(1)}, u32[]{:S(2)}, u32[]{:S(2)}) %all-to-all-start.11) | async-done | bytes 1056 | tf_op jit(solution)/shard_map/all_to_all | solution.py:105
  140.5 3.3 %all-to-all-start.6 = ((f32[1,128,256]{2,0,1:T(1,128)}), f32[1,128,256]{2,0,1:T(1,128)S(1)}, u32[]{:S(2)}, u32[]{:S(2)}) async-start(f32[1,128,256]{2,0,1:T(1,128)} %copy.95), calls=%async_computation.6 | async-start | bytes 262144 | tf_op jit(solution)/shard_map/all_to_all | solution.py:98
  145.1 3.3 %all-to-all-done.6 = f32[1,128,256]{2,0,1:T(1,128)S(1)} async-done(((f32[1,128,256]{2,0,1:T(1,128)}), f32[1,128,256]{2,0,1:T(1,128)S(1)}, u32[]{:S(2)}, u32[]{:S(2)}) %all-to-all-start.6) | async-done | bytes 131104 | tf_op jit(solution)/shard_map/all_to_all | solution.py:98
  148.4 3.5 %all-to-all-start.9 = ((f32[1,64,256]{2,0,1:T(1,128)}), f32[1,64,256]{2,0,1:T(1,128)S(1)}, u32[]{:S(2)}, u32[]{:S(2)}) async-start(f32[1,64,256]{2,0,1:T(1,128)} %copy.104), calls=%async_computation.9 | async-start | bytes 131072 | tf_op jit(solution)/shard_map/all_to_all | solution.py:103
  153.5 3.9 %all-to-all-done.9 = f32[1,64,256]{2,0,1:T(1,128)S(1)} async-done(((f32[1,64,256]{2,0,1:T(1,128)}), f32[1,64,256]{2,0,1:T(1,128)S(1)}, u32[]{:S(2)}, u32[]{:S(2)}) %all-to-all-start.9) | async-done | bytes 65568 | tf_op jit(solution)/shard_map/all_to_all | solution.py:103
  158.9 2.2 %fusion.3 = f32[32,256]{1,0:T(8,128)} fusion(f32[32,256]{1,0:T(8,128)S(1)} %fusion.2, f32[2,512,256]{2,1,0:T(8,128)} %param.26, f32[32,512]{1,0:T(8,128)S(1)} %get-tuple-element.51, f32[512]{0:T(512)S(1)} %bitcast.190, f32[512]{0:T(512)S(1)} %bitcast.192, f32[32]{0:T(128)S(1)} %add_sqrt_fusion.1, f32[32]{0:T(128)S(1)} %broadcast_multiply_fusion.2, ...), kind=kOutput, calls=%fused_computation.17 | convolution fusion | flops 51462144 | bytes 660736 | tf_op jit(solution)/shard_map/dot_general | solution.py:13
  (187 shorter events, 39.7 us)
Async XLA Ops:
  0.6 18.4 %copy-start.2 = (f32[32,256]{1,0:T(8,128)S(1)}, f32[32,256]{1,0:T(8,128)}, u32[]{:S(2)}) copy-start(f32[32,256]{1,0:T(8,128)} %param.14) | copy-start | bytes 98308
  3.5 27.9 %copy-start.11 = (f32[2,512]{1,0:T(2,128)S(1)}, f32[2,512]{1,0:T(2,128)}, u32[]{:S(2)}) copy-start(f32[2,512]{1,0:T(2,128)} %param.23) | copy-start | bytes 12292
  3.5 28.8 %copy-start.12 = (f32[2,512]{1,0:T(2,128)S(1)}, f32[2,512]{1,0:T(2,128)}, u32[]{:S(2)}) copy-start(f32[2,512]{1,0:T(2,128)} %param.25) | copy-start | bytes 12292
  19.0 14.5 %copy-start.13 = (f32[2,512]{1,0:T(2,128)S(1)}, f32[2,512]{1,0:T(2,128)}, u32[]{:S(2)}) copy-start(f32[2,512]{1,0:T(2,128)} %param.24) | copy-start | bytes 12292
  19.0 19.8 %copy-start.14 = (f32[2,256]{1,0:T(2,128)S(1)}, f32[2,256]{1,0:T(2,128)}, u32[]{:S(2)}) copy-start(f32[2,256]{1,0:T(2,128)} %param.21) | copy-start | bytes 6148
  19.0 28.5 %copy-start.15 = (f32[2,256]{1,0:T(2,128)S(1)}, f32[2,256]{1,0:T(2,128)}, u32[]{:S(2)}) copy-start(f32[2,256]{1,0:T(2,128)} %param.27) | copy-start | bytes 6148
  28.1 7.5 %all-to-all-start.2 = ((f32[4,1,128]{2,1,0:T(1,128)}), f32[4,1,128]{2,1,0:T(1,128)S(1)}, u32[]{:S(2)}, u32[]{:S(2)}) async-start(f32[4,1,128]{2,1,0:T(1,128)} %reshape.316), calls=%async_computation.2 | async-start | bytes 4096 | tf_op jit(solution)/shard_map/all_to_all | solution.py:100
  33.5 44.2 %copy-start.1 = (f32[2,256,256]{2,1,0:T(8,128)S(1)}, f32[2,256,256]{2,1,0:T(8,128)}, u32[]{:S(2)}) copy-start(f32[2,256,256]{2,1,0:T(8,128)} %param.20) | copy-start | bytes 1572868
  34.9 43.7 %copy-start = (f32[2,512,512]{2,1,0:T(8,128)S(1)}, f32[2,512,512]{2,1,0:T(8,128)}, u32[]{:S(2)}) copy-start(f32[2,512,512]{2,1,0:T(8,128)} %param.22) | copy-start | bytes 6291460
  35.6 7.0 %all-to-all-start.1 = ((f32[4,1,128]{2,1,0:T(1,128)}), f32[4,1,128]{2,1,0:T(1,128)S(1)}, u32[]{:S(2)}, u32[]{:S(2)}) async-start(f32[4,1,128]{2,1,0:T(1,128)} %reshape.314), calls=%async_computation.1 | async-start | bytes 4096 | tf_op jit(solution)/shard_map/all_to_all | solution.py:99
  42.5 10.6 %all-to-all-start.4 = ((f32[1,64,4]{2,0,1:T(1,128)}), f32[1,64,4]{2,0,1:T(1,128)S(1)}, u32[]{:S(2)}, u32[]{:S(2)}) async-start(f32[1,64,4]{2,0,1:T(1,128)} %copy.85), calls=%async_computation.4 | async-start | bytes 65536 | tf_op jit(solution)/shard_map/all_to_all | solution.py:104
  53.2 8.9 %all-to-all-start.5 = ((f32[1,64,4]{2,0,1:T(1,128)}), f32[1,64,4]{2,0,1:T(1,128)S(1)}, u32[]{:S(2)}, u32[]{:S(2)}) async-start(f32[1,64,4]{2,0,1:T(1,128)} %copy.89), calls=%async_computation.5 | async-start | bytes 65536 | tf_op jit(solution)/shard_map/all_to_all | solution.py:105
  62.1 10.2 %all-to-all-start = ((f32[1,128,256]{2,0,1:T(1,128)}), f32[1,128,256]{2,0,1:T(1,128)}, u32[]{:S(2)}, u32[]{:S(2)}) async-start(f32[1,128,256]{2,0,1:T(1,128)} %copy.75), calls=%async_computation | async-start | bytes 262144 | tf_op jit(solution)/shard_map/all_to_all | solution.py:98
  72.3 9.1 %all-to-all-start.3 = ((f32[1,64,256]{2,0,1:T(1,128)}), f32[1,64,256]{2,0,1:T(1,128)S(1)}, u32[]{:S(2)}, u32[]{:S(2)}) async-start(f32[1,64,256]{2,0,1:T(1,128)} %copy.84), calls=%async_computation.3 | async-start | bytes 131072 | tf_op jit(solution)/shard_map/all_to_all | solution.py:103
  76.5 6.3 %copy-start.3 = (f32[32,256]{1,0:T(8,128)S(1)}, f32[32,256]{1,0:T(8,128)}, u32[]{:S(2)}) copy-start(f32[32,256]{1,0:T(8,128)} %param.14) | copy-start | bytes 98308
  76.6 4.9 %copy-start.5 = (f32[16,4]{1,0:T(8,128)S(1)}, f32[16,4]{1,0:T(8,128)}, u32[]{:S(2)}) copy-start(f32[16,4]{1,0:T(8,128)} %copy.91) | copy-start | bytes 772
  76.6 5.1 %copy-start.10 = (f32[1,256]{1,0:T(1,128)S(1)}, f32[1,256]{1,0:T(1,128)}, u32[]{:S(2)}) copy-start(f32[1,256]{1,0:T(1,128)} %get-tuple-element.39) | copy-start | bytes 3076
  76.6 5.3 %copy-start.8 = (f32[1,512]{1,0:T(1,128)S(1)}, f32[1,512]{1,0:T(1,128)}, u32[]{:S(2)}) copy-start(f32[1,512]{1,0:T(1,128)} %get-tuple-element.35) | copy-start | bytes 6148
  80.2 4.3 %copy-start.18 = (f32[1,512]{1,0:T(1,128)S(1)}, f32[1,512]{1,0:T(1,128)}, u32[]{:S(2)}) copy-start(f32[1,512]{1,0:T(1,128)} %get-tuple-element.33) | copy-start | bytes 6148
  80.2 4.3 %copy-start.19 = (f32[1,512]{1,0:T(1,128)S(1)}, f32[1,512]{1,0:T(1,128)}, u32[]{:S(2)}) copy-start(f32[1,512]{1,0:T(1,128)} %get-tuple-element.31) | copy-start | bytes 6148
  80.2 4.3 %copy-start.21 = (f32[1,256]{1,0:T(1,128)S(1)}, f32[1,256]{1,0:T(1,128)}, u32[]{:S(2)}) copy-start(f32[1,256]{1,0:T(1,128)} %get-tuple-element.37) | copy-start | bytes 3076
  107.7 6.9 %all-to-all-start.8 = ((f32[4,1,128]{2,1,0:T(1,128)}), f32[4,1,128]{2,1,0:T(1,128)S(1)}, u32[]{:S(2)}, u32[]{:S(2)}) async-start(f32[4,1,128]{2,1,0:T(1,128)} %reshape.320), calls=%async_computation.8 | async-start | bytes 4096 | tf_op jit(solution)/shard_map/all_to_all | solution.py:100
  114.6 6.9 %all-to-all-start.7 = ((f32[4,1,128]{2,1,0:T(1,128)}), f32[4,1,128]{2,1,0:T(1,128)S(1)}, u32[]{:S(2)}, u32[]{:S(2)}) async-start(f32[4,1,128]{2,1,0:T(1,128)} %reshape.318), calls=%async_computation.7 | async-start | bytes 4096 | tf_op jit(solution)/shard_map/all_to_all | solution.py:99
  121.5 10.1 %all-to-all-start.10 = ((f32[1,64,4]{2,0,1:T(1,128)}), f32[1,64,4]{2,0,1:T(1,128)S(1)}, u32[]{:S(2)}, u32[]{:S(2)}) async-start(f32[1,64,4]{2,0,1:T(1,128)} %copy.105), calls=%async_computation.10 | async-start | bytes 65536 | tf_op jit(solution)/shard_map/all_to_all | solution.py:104
  126.3 25.9 %copy-start.9 = (f32[1,256]{1,0:T(1,128)S(1)}, f32[1,256]{1,0:T(1,128)}, u32[]{:S(2)}) copy-start(f32[1,256]{1,0:T(1,128)} %get-tuple-element.38) | copy-start | bytes 3076
  131.6 8.9 %all-to-all-start.11 = ((f32[1,64,4]{2,0,1:T(1,128)}), f32[1,64,4]{2,0,1:T(1,128)S(1)}, u32[]{:S(2)}, u32[]{:S(2)}) async-start(f32[1,64,4]{2,0,1:T(1,128)} %copy.109), calls=%async_computation.11 | async-start | bytes 65536 | tf_op jit(solution)/shard_map/all_to_all | solution.py:105
  134.9 17.6 %copy-start.7 = (f32[1,512]{1,0:T(1,128)S(1)}, f32[1,512]{1,0:T(1,128)}, u32[]{:S(2)}) copy-start(f32[1,512]{1,0:T(1,128)} %get-tuple-element.34) | copy-start | bytes 6148
  140.5 7.9 %all-to-all-start.6 = ((f32[1,128,256]{2,0,1:T(1,128)}), f32[1,128,256]{2,0,1:T(1,128)S(1)}, u32[]{:S(2)}, u32[]{:S(2)}) async-start(f32[1,128,256]{2,0,1:T(1,128)} %copy.95), calls=%async_computation.6 | async-start | bytes 262144 | tf_op jit(solution)/shard_map/all_to_all | solution.py:98
  148.4 9.0 %all-to-all-start.9 = ((f32[1,64,256]{2,0,1:T(1,128)}), f32[1,64,256]{2,0,1:T(1,128)S(1)}, u32[]{:S(2)}, u32[]{:S(2)}) async-start(f32[1,64,256]{2,0,1:T(1,128)} %copy.104), calls=%async_computation.9 | async-start | bytes 131072 | tf_op jit(solution)/shard_map/all_to_all | solution.py:103
  151.9 7.0 %copy-start.16 = (f32[1,512]{1,0:T(1,128)S(1)}, f32[1,512]{1,0:T(1,128)}, u32[]{:S(2)}) copy-start(f32[1,512]{1,0:T(1,128)} %get-tuple-element.32) | copy-start | bytes 6148
  151.9 7.0 %copy-start.17 = (f32[1,512]{1,0:T(1,128)S(1)}, f32[1,512]{1,0:T(1,128)}, u32[]{:S(2)}) copy-start(f32[1,512]{1,0:T(1,128)} %get-tuple-element.30) | copy-start | bytes 6148
  151.9 7.0 %copy-start.20 = (f32[1,256]{1,0:T(1,128)S(1)}, f32[1,256]{1,0:T(1,128)}, u32[]{:S(2)}) copy-start(f32[1,256]{1,0:T(1,128)} %get-tuple-element.36) | copy-start | bytes 3076
  (4 other events, 12.1 us)
where the time goes:
time: 164 us; the launch traced here: 162 us
  starting transfers between devices  42.9 us (26%)
  blocking collectives  40.5 us (25%)
  waiting for transfers between devices  28 us (17%)
  local copies, waits for them, and re-layouts  24.7 us (15%)
  matrix products  14.4 us (9%)
  other arithmetic  10.1 us (6%)
    all_gather x2, blocking collectives, shards(): block_b = lax.all_gather(proj_b, 'aa', axis=0, tiled=True)  28.4 us
    dot_general x16, matrix products, matmul(): return jnp.dot(left, right, precision=EXACT_RESULT)  12.3 us
    all_gather x2, blocking collectives, shards(): block_a = lax.all_gather(proj_a, 'ba', axis=0, tiled=True)  12 us
    all_to_all x2, starting transfers between devices, shards(): lax.all_to_all(col_tops[None], 'aa', split_axis=1, concat_axis=0, tiled=T...  9.41 us
    all_to_all x2, waiting for transfers between devices, shards(): lax.all_to_all(col_tops[None], 'aa', split_axis=1, concat_axis=0, tiled=T...  8.91 us
    all_to_all x2, starting transfers between devices, shards(): lax.all_to_all(numer_a[None], 'ba', split_axis=1, concat_axis=0, tiled=True)  7.26 us
    all_to_all x2, starting transfers between devices, shards(): lax.all_to_all(numer_b[None], 'aa', split_axis=1, concat_axis=0, tiled=True)  6.82 us
    all_to_all x2, starting transfers between devices, shards(): lax.all_to_all(col_totals[None], 'aa', split_axis=1, concat_axis=0, tiled...  6.53 us
  transfers between devices with their start and end apart: 12, of which 10 were waited for; matrix products, arithmetic and copies ran while one was open for 19% of the time, Pallas kernels for 0%

commit v1 on v0

v1 whole, which is shorter than its diff:
```python
import functools

import jax
import jax.numpy as jnp
from jax import lax
from jax.experimental import pallas as pl
from jax.experimental.pallas import tpu as pltpu
from jax.sharding import PartitionSpec as P

HEADS = 4
LANES = 128
F32 = jnp.float32
BF16 = jnp.bfloat16
NN = (((1,), (0,)), ((), ()))
NT = (((1,), (1,)), ((), ()))


def split(x):
    hi = x.astype(BF16)
    return hi, (x - hi.astype(F32)).astype(BF16)


def dot3(a, b, dims=NN):
    f = functools.partial(lax.dot_general, dimension_numbers=dims, preferred_element_type=F32)
    return f(a[0], b[0]) + (f(a[1], b[0]) + f(a[0], b[1]))


def erf(x):
    x = jnp.clip(x, -3.832506856900711, 3.832506856900711)
    z = x * x
    p = jnp.full_like(z, 0.00022905065861350646)
    for c in (0.0034082910107109506, 0.050955695062380861, 0.18520832239976145, 1.128379143519084):
        p = p * z + c
    q = jnp.full_like(z, -1.1791602954361697e-7)
    for c in (
        0.000023547966471313185,
        0.0010179625278914885,
        0.014070470171167667,
        0.11098505178285362,
        0.49746925110067538,
        1.0,
    ):
        q = q * z + c
    return x * p / q


def head_masks(width):
    lane = lax.broadcasted_iota(jnp.int32, (1, width), 1)
    size = width // HEADS
    return [(lane >= h * size) & (lane < (h + 1) * size) for h in range(HEADS)]


def attend(q, k, v, scale):
    width = q[0].shape[1]
    cols = k[0].shape[0]
    ones = [m.astype(F32).astype(BF16) for m in head_masks(width)]
    kb = [jnp.concatenate([part * m for m in ones], 0) for part in k]
    vb = [jnp.concatenate([part * m for m in ones], 0) for part in v]
    s = dot3(q, kb, NT) * scale
    lane = lax.broadcasted_iota(jnp.int32, (1, LANES), 1)
    stats = jnp.zeros((s.shape[0], LANES), F32)
    if cols % LANES == 0:
        parts = []
        for h in range(HEADS):
            sh = s[:, h * cols : (h + 1) * cols]
            top = jnp.max(sh, 1, keepdims=True)
            e = jnp.exp(sh - top)
            total = jnp.sum(e, 1, keepdims=True)
            parts.append(e)
            stats = jnp.where(lane == h, top, jnp.where(lane == HEADS + h, total, stats))
        e = jnp.concatenate(parts, 1)
    else:
        masks = head_masks(s.shape[1])
        shift = jnp.zeros_like(s)
        for h in range(HEADS):
            top = jnp.max(jnp.where(masks[h], s, -jnp.inf), 1, keepdims=True)
            shift = jnp.where(masks[h], top, shift)
            stats = jnp.where(lane == h, top, stats)
        e = jnp.exp(s - shift)
        for h in range(HEADS):
            total = jnp.sum(jnp.where(masks[h], e, 0.0), 1, keepdims=True)
            stats = jnp.where(lane == HEADS + h, total, stats)
    return dot3(split(e), vb), stats


def settle(got, layer):
    sources, rows, packed = got.shape[1:]
    width = packed - LANES
    masks = head_masks(width)
    stats = [got[layer, i, :, width:] for i in range(sources)]
    best = functools.reduce(jnp.maximum, stats)
    weights = [jnp.exp(st - best) for st in stats]
    denom = sum(w * pltpu.roll(st, LANES - HEADS, 1) for w, st in zip(weights, stats))
    out = jnp.zeros((rows, width), F32)
    for i in range(sources):
        c = weights[i] / denom
        full = jnp.zeros((rows, width), F32)
        for h in range(HEADS):
            full = jnp.where(masks[h], c[:, h : h + 1], full)
        out = out + full * got[layer, i, :, :width]
    return out


def kernel(na, nb, *refs):
    (fa, fb), weights, (out_a, out_b) = refs[:2], refs[2:14], refs[14:16]
    (xa, xb, sa, sb, ga, gb), rest = refs[16:22], refs[22:]
    held, rest = rest[:12], rest[12:]
    his, los = rest[:5], rest[5:10]
    load, in_sem, xs, xr, ys, yr, ps, pr, qs, qr = rest[10:]
    wqk, bqk, wv, bv, wo, bo, wh, bh, gain, nbias, wf, bf = held
    layers, _, ra, width = xa.shape
    rb = xb.shape[2]
    scale = (width // HEADS) ** (-0.5)
    ma, mb = lax.axis_index("ba"), lax.axis_index("aa")

    first = [
        pltpu.make_async_copy(fa, xa.at[0, ma], in_sem.at[0]),
        pltpu.make_async_copy(fb, xb.at[0, mb], in_sem.at[1]),
    ]
    for c in first:
        c.start()
    loads = [pltpu.make_async_copy(w, h, load.at[i]) for i, (w, h) in enumerate(zip(weights, held))]
    for c in loads:
        c.start()

    barrier = pltpu.get_barrier_semaphore()
    for axis, me, n in (("ba", ma, nb), ("aa", mb, na)):
        for d in range(1, n):
            pl.semaphore_signal(
                barrier,
                inc=1,
                device_id={axis: (me + d) % n},
                device_id_type=pl.DeviceIdType.MESH,
            )
    pl.semaphore_wait(barrier, na + nb - 2)
    for c in first:
        c.wait()

    sent = []

    def exchange(axis, me, n, source, target, layer, ssem, rsem):
        arrive = []
        for d in range(1, n):
            peer = (me + d) % n
            copy = pltpu.make_async_remote_copy(
                src_ref=source(peer),
                dst_ref=target.at[layer, me],
                send_sem=ssem.at[layer, d],
                recv_sem=rsem.at[layer, me],
                device_id={axis: peer},
                device_id_type=pl.DeviceIdType.MESH,
            )
            copy.start()
            sent.append(copy)
            arrive.append(
                pltpu.make_async_remote_copy(
                    src_ref=target.at[layer, peer],
                    dst_ref=target.at[layer, peer],
                    send_sem=ssem.at[layer, d],
                    recv_sem=rsem.at[layer, peer],
                    device_id={axis: peer},
                    device_id_type=pl.DeviceIdType.MESH,
                )
            )
        return arrive

    matrices = (wqk, wv, wo, wh, wf)

    def narrow(which, layer):
        for i in which:
            his[i][layer], los[i][layer] = split(matrices[i][layer])

    def wide(i, layer):
        return his[i][layer], los[i][layer]

    for l in range(layers):
        arrive = exchange("aa", mb, na, lambda p: xb.at[l, mb], xb, l, ys, yr)
        arrive += exchange("ba", ma, nb, lambda p: xa.at[l, ma], xa, l, xs, xr)
        if l == 0:
            for c in loads:
                c.wait()
            narrow(range(5), 0)
        for c in arrive:
            c.wait_recv()
        rows_a = split(xa[l].reshape(nb * ra, width))
        rows_b = split(xb[l].reshape(na * rb, width))
        w, u = wide(0, l), wide(1, l)
        qa = split(dot3(rows_a, w) + bqk[l : l + 1])
        va = split(dot3(rows_a, u) + bv[l : l + 1])
        qb = split(dot3(rows_b, w) + bqk[l : l + 1])
        vb = split(dot3(rows_b, u) + bv[l : l + 1])

        numer, stats = attend(qb, qa, va, scale)
        sb[l, :, :, :width] = numer.reshape(na, rb, width)
        sb[l, :, :, width:] = stats.reshape(na, rb, LANES)
        arrive = exchange("aa", mb, na, lambda p: sb.at[l, p], gb, l, qs, qr)
        numer, stats = attend(qa, qb, vb, scale)
        sa[l, :, :, :width] = numer.reshape(nb, ra, width)
        sa[l, :, :, width:] = stats.reshape(nb, ra, LANES)
        arrive += exchange("ba", ma, nb, lambda p: sa.at[l, p], ga, l, ps, pr)
        ga[l, ma] = sa[l, ma]
        gb[l, mb] = sb[l, mb]
        if l + 1 < layers:
            narrow(range(5), l + 1)
        for c in arrive:
            c.wait_recv()

        x = jnp.concatenate([xa[l, ma], xb[l, mb]], 0)
        msg = jnp.concatenate([settle(ga, l), settle(gb, l)], 0)
        y = dot3(split(msg), wide(2, l)) + bo[l : l + 1]
        joined = split(jnp.concatenate([x, y], 1))
        hidden = dot3(joined, wide(3, l)) + bh[l : l + 1]
        centred = hidden - jnp.mean(hidden, 1, keepdims=True)
        spread = jnp.mean(centred * centred, 1, keepdims=True)
        normed = centred / jnp.sqrt(spread + 1e-05) * gain[l : l + 1] + nbias[l : l + 1]
        active = 0.5 * normed * (1.0 + erf(normed * (0.5**0.5)))
        x = x + dot3(split(active), wide(4, l)) + bf[l : l + 1]
        if l + 1 < layers:
            xa[l + 1, ma] = x[:ra]
            xb[l + 1, mb] = x[ra:]
        else:
            out_a[...] = x[:ra]
            out_b[...] = x[ra:]
    for c in sent:
        c.wait_send()


def shards(na, nb, *args):
    fa, fb, *weights = args
    layers = weights[0].shape[0]
    (ra, width), rb = fa.shape, fb.shape[0]
    packed = width + LANES
    matrices = [weights[i] for i in (0, 2, 4, 6, 10)]
    dma = pltpu.SemaphoreType.DMA
    scratch = [
        pltpu.VMEM((layers, nb, ra, width), F32),
        pltpu.VMEM((layers, na, rb, width), F32),
        pltpu.VMEM((layers, nb, ra, packed), F32),
        pltpu.VMEM((layers, na, rb, packed), F32),
        pltpu.VMEM((layers, nb, ra, packed), F32),
        pltpu.VMEM((layers, na, rb, packed), F32),
    ]
    scratch += [pltpu.VMEM(w.shape, F32) for w in weights]
    scratch += [pltpu.VMEM(w.shape, BF16) for w in matrices] * 2
    scratch += [dma((len(weights),)), dma((2,))]
    scratch += [dma((layers, n)) for n in (nb, nb, na, na, nb, nb, na, na)]
    any_spec = pl.BlockSpec(memory_space=pl.ANY)
    vmem = pl.BlockSpec(memory_space=pltpu.VMEM)
    return tuple(
        pl.pallas_call(
            functools.partial(kernel, na, nb),
            out_shape=(
                jax.ShapeDtypeStruct(fa.shape, F32),
                jax.ShapeDtypeStruct(fb.shape, F32),
            ),
            in_specs=[any_spec] * len(args),
            out_specs=(vmem, vmem),
            scratch_shapes=scratch,
            compiler_params=pltpu.CompilerParams(
                collective_id=0, has_side_effects=True, vmem_limit_bytes=60 * 1024 * 1024
            ),
        )(*args)
    )


def solution(mesh):
    in_specs = (P(("pairs", "aa", "ba"), None), P(("pairs", "ba", "aa"), None)) + (P(),) * 12
    out_specs = (P(("pairs", "aa", "ba"), None), P(("pairs", "ba", "aa"), None))
    return jax.shard_map(
        functools.partial(shards, mesh.shape["aa"], mesh.shape["ba"]),
        mesh=mesh,
        in_specs=in_specs,
        out_specs=out_specs,
        check_vma=False,
    )
```

time: 164 us -> 30.7 us (0.19)
  starting transfers between devices: 42.9 us -> 0 us
  blocking collectives: 40.5 us -> 0 us
  waiting for transfers between devices: 28 us -> 0 us
  Pallas kernels: 0 us -> 27.1 us
  local copies, waits for them, and re-layouts: 24.7 us -> 2.7 us
  matrix products: 14.4 us -> 0 us
  other arithmetic: 10.1 us -> 0 us
    all_to_all x12 -> x0, starting transfers between devices: 42.9 us -> none  [the longest x2 9.41 us: shards(): lax.all_to_all(col_tops[None], 'aa', split_axis=1, concat_axis=0, tiled=T...]
    all_gather x4 -> x0, blocking collectives: 40.5 us -> none  [the longest x2 28.4 us: shards(): block_b = lax.all_gather(proj_b, 'aa', axis=0, tiled=True)]
    all_to_all x12 -> x0, waiting for transfers between devices: 28 us -> none  [the longest x2 8.91 us: shards(): lax.all_to_all(col_tops[None], 'aa', split_axis=1, concat_axis=0, tiled=T...]
    pallas_call x0 -> x1, Pallas kernels: none -> 27.1 us  [shards(): pl.pallas_call(functools.partial(kernel, na, nb), out_shape=(jax.ShapeDty...]
    dot_general x22 -> x0, matrix products: 14.4 us -> none  [the longest x16 12.3 us: matmul(): return jnp.dot(left, right, precision=EXACT_RESULT)]
    slice x15 -> x0, local copies, waits for them, and re-layouts: 4.9 us -> none  [the longest x1 0.76 us: shards(): value_bias[layer_index]]
    broadcast_in_dim x8 -> x0, local copies, waits for them, and re-layouts: 3.27 us -> none  [the longest x2 1.42 us: shards(): col_totals[None]]
    reduce_sum x8 -> x0, local copies, waits for them, and re-layouts: 3.21 us -> none  [the longest x4 2.87 us: settle_owner(): denom = jnp.sum(weight * totals, 0)]
  transfers between devices with their start and end apart: 12 -> 0, of which waited for: 10 -> 0; matrix products, arithmetic and copies ran while one was open for 19% -> 0% of each run, Pallas kernels for 0% -> 0%
where the time goes in v1:
time: 30.7 us; the launch traced here: 30.4 us
  Pallas kernels  27.1 us (88%)
  local copies, waits for them, and re-layouts  2.7 us (9%)
  between operations  0.64 us (2%)
    pallas_call x1, Pallas kernels, shards(): pl.pallas_call(functools.partial(kernel, na, nb), out_shape=(jax.ShapeDty...  27.1 us
    unnamed x2, local copies, waits for them, and re-layouts  2.7 us

profile of v1, /device:TPU:0, one launch (start us, length us, event | category | flops | bytes accessed | tf_op | source)
XLA Modules:
  0.0 30.4 jit_solution(15046390417426939986)
XLA Ops:
  0.6 27.1 %shard_map.149 = (f32[32,256]{1,0:T(8,128)}, f32[16,256]{1,0:T(8,128)}) custom-call(f32[32,256]{1,0:T(8,128)} %refs_0_.1, f32[16,256]{1,0:T(8,128)} %refs_1_.1, f32[2,256,256]{2,1,0:T(8,128)} %refs_2_.1, f32[2,256]{1,0:T(2,128)} %refs_3_.1, f32[2,256,256]{2,1,0:T(8,128)} %refs_4_.1, f32[2,256]{1,0:T(2,128)} %refs_5_.1, f32[2,256,256]{2,1,0:T(8,128)} %refs_6_.1, ...), custom_call_target="tpu_custom_call" | custom-call | tf_op jit(solution)/shard_map/pallas_call | solution.py:250
  27.7 1.4 %copy.18 = f32[32,256]{1,0:T(8,128)} copy(f32[32,256]{1,0:T(8,128)} %get-tuple-element.4) | data formatting | bytes 65536
  29.1 1.3 %copy.19 = f32[16,256]{1,0:T(8,128)} copy(f32[16,256]{1,0:T(8,128)} %get-tuple-element.5) | data formatting | bytes 32768

commit v2 on v1

--- a/solution.py
+++ b/solution.py
@@ -106,7 +106,7 @@
     (xa, xb, sa, sb, ga, gb), rest = refs[16:22], refs[22:]
     held, rest = rest[:12], rest[12:]
     his, los = rest[:5], rest[5:10]
-    load, in_sem, xs, xr, ys, yr, ps, pr, qs, qr = rest[10:]
+    load, vec, in_sem, xs, xr, ys, yr, ps, pr, qs, qr = rest[10:]
     wqk, bqk, wv, bv, wo, bo, wh, bh, gain, nbias, wf, bf = held
     layers, _, ra, width = xa.shape
     rb = xb.shape[2]
@@ -119,9 +119,18 @@
     ]
     for c in first:
         c.start()
-    loads = [pltpu.make_async_copy(w, h, load.at[i]) for i, (w, h) in enumerate(zip(weights, held))]
-    for c in loads:
+    small = [(w, h) for w, h in zip(weights, held) if len(w.shape) == 2]
+    large = [(w, h) for w, h in zip(weights, held) if len(w.shape) == 3]
+    vectors = [pltpu.make_async_copy(w, h, vec.at[i]) for i, (w, h) in enumerate(small)]
+    loads = [
+        [pltpu.make_async_copy(w.at[j], h.at[j], load.at[j, i]) for i, (w, h) in enumerate(large)]
+        for j in range(layers)
+    ]
+    for c in loads[0][:2] + vectors + loads[0][2:]:
         c.start()
+    for later in loads[1:]:
+        for c in later:
+            c.start()
 
     barrier = pltpu.get_barrier_semaphore()
     for axis, me, n in (("ba", ma, nb), ("aa", mb, na)):
@@ -168,25 +177,28 @@
 
     def narrow(which, layer):
         for i in which:
+            loads[layer][i].wait()
             his[i][layer], los[i][layer] = split(matrices[i][layer])
 
     def wide(i, layer):
         return his[i][layer], los[i][layer]
 
     for l in range(layers):
-        arrive = exchange("aa", mb, na, lambda p: xb.at[l, mb], xb, l, ys, yr)
-        arrive += exchange("ba", ma, nb, lambda p: xa.at[l, ma], xa, l, xs, xr)
+        far = exchange("aa", mb, na, lambda p: xb.at[l, mb], xb, l, ys, yr)
+        near = exchange("ba", ma, nb, lambda p: xa.at[l, ma], xa, l, xs, xr)
         if l == 0:
-            for c in loads:
+            narrow(range(2), 0)
+            for c in vectors:
                 c.wait()
-            narrow(range(5), 0)
-        for c in arrive:
+        for c in near:
             c.wait_recv()
         rows_a = split(xa[l].reshape(nb * ra, width))
-        rows_b = split(xb[l].reshape(na * rb, width))
         w, u = wide(0, l), wide(1, l)
         qa = split(dot3(rows_a, w) + bqk[l : l + 1])
         va = split(dot3(rows_a, u) + bv[l : l + 1])
+        for c in far:
+            c.wait_recv()
+        rows_b = split(xb[l].reshape(na * rb, width))
         qb = split(dot3(rows_b, w) + bqk[l : l + 1])
         vb = split(dot3(rows_b, u) + bv[l : l + 1])
 
@@ -200,8 +212,10 @@
         arrive += exchange("ba", ma, nb, lambda p: sa.at[l, p], ga, l, ps, pr)
         ga[l, ma] = sa[l, ma]
         gb[l, mb] = sb[l, mb]
-        if l + 1 < layers:
-            narrow(range(5), l + 1)
+        if l == 0:
+            narrow(range(2, 5), 0)
+            for j in range(1, layers):
+                narrow(range(5), j)
         for c in arrive:
             c.wait_recv()
 
@@ -242,16 +256,16 @@
     ]
     scratch += [pltpu.VMEM(w.shape, F32) for w in weights]
     scratch += [pltpu.VMEM(w.shape, BF16) for w in matrices] * 2
-    scratch += [dma((len(weights),)), dma((2,))]
+    scratch += [dma((layers, len(matrices))), dma((len(weights) - len(matrices),)), dma((2,))]
     scratch += [dma((layers, n)) for n in (nb, nb, na, na, nb, nb, na, na)]
-    any_spec = pl.BlockSpec(memory_space=pl.ANY)
+    any_spec = pl.BlockSpec(memory_space=pltpu.HBM)
     vmem = pl.BlockSpec(memory_space=pltpu.VMEM)
     return tuple(
         pl.pallas_call(
             functools.partial(kernel, na, nb),
             out_shape=(
-                jax.ShapeDtypeStruct(fa.shape, F32),
-                jax.ShapeDtypeStruct(fb.shape, F32),
+                pltpu.VMEM(fa.shape, F32),
+                pltpu.VMEM(fb.shape, F32),
             ),
             in_specs=[any_spec] * len(args),
             out_specs=(vmem, vmem),

time: 30.7 us -> 28.4 us (0.925)
  local copies, waits for them, and re-layouts: 2.7 us -> 1.22 us
  Pallas kernels: 27.1 us -> 26.4 us
    unnamed x2, local copies, waits for them, and re-layouts: 2.7 us -> 1.22 us
    pallas_call x1, Pallas kernels: 27.1 us -> 26.4 us  [shards(): pl.pallas_call(functools.partial(kernel, na, nb), out_shape=(pltpu.VMEM(f...]
where the time goes in v2:
time: 28.4 us; the launch traced here: 28.3 us
  Pallas kernels  26.4 us (93%)
  local copies, waits for them, and re-layouts  1.22 us (4%)
  between operations  0.64 us (2%)
    pallas_call x1, Pallas kernels, shards(): pl.pallas_call(functools.partial(kernel, na, nb), out_shape=(pltpu.VMEM(f...  26.4 us
    unnamed x2, local copies, waits for them, and re-layouts  1.22 us

profile of v2, /device:TPU:0, one launch (start us, length us, event | category | flops | bytes accessed | tf_op | source)
XLA Modules:
  0.0 28.3 jit_solution(10154669976372184479)
XLA Ops:
  0.6 26.4 %shard_map.149 = (f32[32,256]{1,0:T(8,128)S(1)}, f32[16,256]{1,0:T(8,128)S(1)}) custom-call(f32[32,256]{1,0:T(8,128)} %refs_0_.1, f32[16,256]{1,0:T(8,128)} %refs_1_.1, f32[2,256,256]{2,1,0:T(8,128)} %refs_2_.1, f32[2,256]{1,0:T(2,128)} %refs_3_.1, f32[2,256,256]{2,1,0:T(8,128)} %refs_4_.1, f32[2,256]{1,0:T(2,128)} %refs_5_.1, f32[2,256,256]{2,1,0:T(8,128)} %refs_6_.1, ...), custom_call_target="tpu_custom_call" | custom-call | tf_op jit(solution)/shard_map/pallas_call | solution.py:264
  27.0 0.6 %copy.18 = f32[32,256]{1,0:T(8,128)} copy(f32[32,256]{1,0:T(8,128)S(1)} %get-tuple-element.2) | data formatting | bytes 65536
  27.7 0.6 %copy.19 = f32[16,256]{1,0:T(8,128)} copy(f32[16,256]{1,0:T(8,128)S(1)} %get-tuple-element.3) | data formatting | bytes 32768

commit v3 on v2

--- a/solution.py
+++ b/solution.py
@@ -99,6 +99,12 @@
             full = jnp.where(masks[h], c[:, h : h + 1], full)
         out = out + full * got[layer, i, :, :width]
     return out
+
+
+def far_first(me, k, n):
+    up = k + jnp.where(k >= me, 1, 0)
+    down = n - 1 - k - jnp.where(n - 1 - k <= me, 1, 0)
+    return jnp.where(me < n // 2, down, up)
 
 
 def kernel(na, nb, *refs):
@@ -150,7 +156,7 @@
     def exchange(axis, me, n, source, target, layer, ssem, rsem):
         arrive = []
         for d in range(1, n):
-            peer = (me + d) % n
+            peer = far_first(me, d - 1, n) if axis == "aa" else (me + d) % n
             copy = pltpu.make_async_remote_copy(
                 src_ref=source(peer),
                 dst_ref=target.at[layer, me],

time: 28.4 us -> 28.1 us (0.989)
  Pallas kernels: 26.4 us -> 26.1 us
    pallas_call x1, Pallas kernels: 26.4 us -> 26.1 us  [shards(): pl.pallas_call(functools.partial(kernel, na, nb), out_shape=(pltpu.VMEM(f...]
where the time goes in v3:
time: 28.1 us; the launch traced here: 27.9 us
  Pallas kernels  26.1 us (93%)
  local copies, waits for them, and re-layouts  1.22 us (4%)
  between operations  0.64 us (2%)
    pallas_call x1, Pallas kernels, shards(): pl.pallas_call(functools.partial(kernel, na, nb), out_shape=(pltpu.VMEM(f...  26.1 us
    unnamed x2, local copies, waits for them, and re-layouts  1.22 us

profile of v3, /device:TPU:0, one launch (start us, length us, event | category | flops | bytes accessed | tf_op | source)
XLA Modules:
  0.0 27.9 jit_solution(14332675335353070143)
XLA Ops:
  0.6 26.1 %shard_map.149 = (f32[32,256]{1,0:T(8,128)S(1)}, f32[16,256]{1,0:T(8,128)S(1)}) custom-call(f32[32,256]{1,0:T(8,128)} %refs_0_.1, f32[16,256]{1,0:T(8,128)} %refs_1_.1, f32[2,256,256]{2,1,0:T(8,128)} %refs_2_.1, f32[2,256]{1,0:T(2,128)} %refs_3_.1, f32[2,256,256]{2,1,0:T(8,128)} %refs_4_.1, f32[2,256]{1,0:T(2,128)} %refs_5_.1, f32[2,256,256]{2,1,0:T(8,128)} %refs_6_.1, ...), custom_call_target="tpu_custom_call" | custom-call | tf_op jit(solution)/shard_map/pallas_call | solution.py:270
  26.7 0.6 %copy.18 = f32[32,256]{1,0:T(8,128)} copy(f32[32,256]{1,0:T(8,128)S(1)} %get-tuple-element.2) | data formatting | bytes 65536
  27.3 0.6 %copy.19 = f32[16,256]{1,0:T(8,128)} copy(f32[16,256]{1,0:T(8,128)S(1)} %get-tuple-element.3) | data formatting | bytes 32768
